TPU v7x, 32 devices: a whole 2x2x4 slice. The times are simulated.
32 devices in a mesh: grp: 2 (over x), tile: 16 (over z, y, core).
Axes of the slice: x: 2, y: 2, z: 4, core: 2. Of those that a mesh axis runs over, the one named last changes fastest.
Arguments:
- quantized: bfloat16 [16, 96, 2048], P(None, 'grp', 'tile'), may hold values from -6 to 6
- scales: float32 [16, 16, 96], P('tile', None, 'grp'), may hold values from 0.25 to 4
Outputs:
- coefficients: bfloat16 [16, 96, 2048], P(None, 'grp', 'tile')
All inputs are finite; a program needn't handle non-finite values.
Results may differ from a plain program's by a relative error of at most 0.001.
Values sent between devices are 32-bit elements; how exact they have to be, the bound alone decides.
No kernel may reach another device: no remote copies, remote signals or barrier semaphores. Data moves between devices by JAX's collectives and lax.ppermute only.
A program may use at most 64 MiB of HBM per device.

v0:
```python
import jax
import jax.numpy as jnp
from jax import lax
from jax.sharding import PartitionSpec as P

QB = 128
LEVELS = 4


LIFT_ALPHA = -1.586134342059924
LIFT_BETA = -0.052980118572961
LIFT_GAMMA = 0.882911075530934
LIFT_DELTA = 0.443506852043971
LIFT_KAPPA = 1.230174104914001
HIGHEST = lax.Precision.HIGHEST


def padded(x, sides, width):
    for axis, dim in sides:
        size, length = (lax.axis_size(axis), x.shape[dim])
        up = [(i, (i + 1) % size) for i in range(size - 1)]
        down = [(j, i) for i, j in up]
        last = lax.slice_in_dim(x, length - width, length, axis=dim)
        initial = lax.slice_in_dim(x, 0, width, axis=dim)
        before = lax.ppermute(last, axis, up)
        after = lax.ppermute(initial, axis, down)
        x = jnp.concatenate([before, x, after], axis=dim)
    return x


def forward_of(values, along):
    length = values.shape[along]
    return jnp.concatenate(
        [
            lax.slice_in_dim(values, 1, length, 1, along),
            lax.slice_in_dim(values, length - 1, length, 1, along),
        ],
        along,
    )


def backward_of(values, along):
    length = values.shape[along]
    return jnp.concatenate(
        [
            lax.slice_in_dim(values, 0, 1, 1, along),
            lax.slice_in_dim(values, 0, length - 1, 1, along),
        ],
        along,
    )


def lift_local(subband, along):
    length = subband.shape[along]
    even_part = lax.slice_in_dim(subband, 0, length, 2, along)
    odd_part = lax.slice_in_dim(subband, 1, length, 2, along)
    odd_part = odd_part + LIFT_ALPHA * (even_part + forward_of(even_part, along))
    even_part = even_part + LIFT_BETA * (backward_of(odd_part, along) + odd_part)
    odd_part = odd_part + LIFT_GAMMA * (even_part + forward_of(even_part, along))
    even_part = even_part + LIFT_DELTA * (backward_of(odd_part, along) + odd_part)
    even_part = even_part / LIFT_KAPPA
    odd_part = odd_part * (LIFT_KAPPA / 2.0)
    return jnp.stack([even_part, odd_part], along + 1).reshape(subband.shape)


def lift_matrix(length):
    return lift_local(jnp.eye(length, dtype=jnp.float32), 0)


def apply_along(values, matrix, along):
    if along == 2:
        return jnp.dot(values, matrix.T, precision=HIGHEST)
    if along == 1:
        return jnp.einsum("wy,zyx->zwx", matrix, values, precision=HIGHEST)
    flat = values.reshape(values.shape[0], -1)
    result = jnp.dot(matrix, flat, precision=HIGHEST)
    return result.reshape((matrix.shape[0],) + values.shape[1:])


def mirror_edges(widened, along, devices, position):
    length = widened.shape[along] - 8
    middle = lax.slice_in_dim(widened, 4, 4 + length, 1, along)
    left_rim = jnp.where(
        position == 0,
        jnp.flip(lax.slice_in_dim(widened, 5, 9, 1, along), along),
        lax.slice_in_dim(widened, 0, 4, 1, along),
    )
    right_rim = jnp.where(
        position == devices - 1,
        jnp.flip(lax.slice_in_dim(widened, length - 1, length + 3, 1, along), along),
        lax.slice_in_dim(widened, length + 4, length + 8, 1, along),
    )
    return jnp.concatenate([left_rim, middle, right_rim], along)


def lift_plane(subband):
    rows_here = subband.shape[1]
    columns = subband.shape[2]
    extended = padded(subband, (("grp", 1), ("tile", 2)), 4)
    extended = mirror_edges(extended, 2, lax.axis_size("tile"), lax.axis_index("tile"))
    across = apply_along(extended, lift_matrix(columns + 8)[4 : 4 + columns], 2)
    across = mirror_edges(across, 1, lax.axis_size("grp"), lax.axis_index("grp"))
    return apply_along(across, lift_matrix(rows_here + 8)[4 : 4 + rows_here], 1)


def decompose(subband, level_index):
    subband = lift_plane(subband)
    subband = apply_along(subband, lift_matrix(subband.shape[0]), 0)
    if level_index + 1 < LEVELS:
        coarser = decompose(subband[::2, ::2, ::2], level_index + 1)
        subband = subband.at[::2, ::2, ::2].set(coarser)
    return subband


def body(quantized, scales):
    planes, rows_here, columns = quantized.shape
    blocks = quantized.astype(jnp.float32).reshape(planes, rows_here, columns // QB, QB)
    factor = jnp.transpose(scales, (1, 2, 0))[..., None]
    density = (blocks * factor).reshape(planes, rows_here, columns)
    return decompose(density, 0).astype(jnp.bfloat16)


def solution(mesh):
    return jax.shard_map(
        body,
        mesh=mesh,
        in_specs=(P(None, "grp", "tile"), P("tile", None, "grp")),
        out_specs=P(None, "grp", "tile"),
        check_vma=False,
    )
```

profile of v0, /device:TPU:21, one launch (start us, length us, event | category | flops | bytes accessed | tf_op | source)
XLA Modules:
  0.0 158.7 jit_solution(2167701906682247223)
XLA Ops:
  0.0 1.1 convert_multiply_fusion
  1.1 1.3 collective-permute-start.1
  2.4 4.0 %collective-permute-start = (f32[16,4,128]{2,1,0:T(4,128)S(1)}, f32[16,4,128]{2,1,0:T(4,128)S(1)}, u32[]{:S(2)}, u32[]{:S(2)}) collective-permute-start(f32[16,4,128]{2,1,0:T(4,128)S(1)} %get-tuple-element.35), channel_id=1, source_target_pairs={{0,16},{1,17},{2,18},{3,19},{4,20},{5,21},{6,22},{7,23},{8,24},{9,... | collective-permute-start | bytes 98312 | tf_op jit(solution)/shard_map/ppermute | solution.py:25
  6.7 1.3 slice.606
  8.0 1.3 slice.605
  11.3 0.6 copy-done.13
  12.6 0.6 multiply_bitcast_fusion.3
  13.5 0.6 copy-done.12
  14.2 0.5 copy-done.11
  14.9 0.6 multiply_bitcast_fusion.4
  15.5 0.6 fusion.174
  16.3 0.6 multiply_bitcast_fusion.6
  17.3 0.6 fusion.161
  18.0 0.6 fusion.150
  18.8 0.5 copy-done
  19.8 3.1 %collective-permute-start.3 = (f32[16,56,4]{2,1,0:T(8,128)S(1)}, f32[16,56,4]{2,1,0:T(8,128)S(1)}, u32[]{:S(2)}, u32[]{:S(2)}) collective-permute-start(f32[16,56,4]{2,1,0:T(8,128)S(1)} %get-tuple-element.32), channel_id=1, source_target_pairs={{1,0},{2,1},{3,2},{4,3},{5,4},{6,5},{7,6},{8,7},{9,8},{10,9},{11,1... | collective-permute-start | bytes 43016 | tf_op jit(solution)/shard_map/ppermute | solution.py:26
  23.2 0.6 stack.139
  23.8 0.6 copy.81
  24.7 3.3 %collective-permute-start.2 = (f32[16,56,4]{2,1,0:T(8,128)S(1)}, f32[16,56,4]{2,1,0:T(8,128)S(1)}, u32[]{:S(2)}, u32[]{:S(2)}) collective-permute-start(f32[16,56,4]{2,1,0:T(8,128)S(1)} %get-tuple-element.31), channel_id=1, source_target_pairs={{0,1},{1,2},{2,3},{3,4},{4,5},{5,6},{6,7},{7,8},{8,9},{9,10},{10,1... | collective-permute-start | bytes 43016 | tf_op jit(solution)/shard_map/ppermute | solution.py:25
  28.1 2.5 %collective-permute-done.3 = f32[16,56,4]{2,1,0:T(8,128)S(1)} collective-permute-done((f32[16,56,4]{2,1,0:T(8,128)S(1)}, f32[16,56,4]{2,1,0:T(8,128)S(1)}, u32[]{:S(2)}, u32[]{:S(2)}) %collective-permute-start.3) | collective-permute-done | bytes 14368 | tf_op jit(solution)/shard_map/ppermute | solution.py:26
  30.6 2.9 %collective-permute-done.2 = f32[16,56,4]{2,1,0:T(8,128)S(1)} collective-permute-done((f32[16,56,4]{2,1,0:T(8,128)S(1)}, f32[16,56,4]{2,1,0:T(8,128)S(1)}, u32[]{:S(2)}, u32[]{:S(2)}) %collective-permute-start.2) | collective-permute-done | bytes 14368 | tf_op jit(solution)/shard_map/ppermute | solution.py:25
  33.5 1.1 fusion
  34.8 0.6 fusion.10
  36.0 3.5 %slice.644 = f32[8,24,64]{2,0,1:T(8,128)S(1)} slice(f32[16,48,128]{2,0,1:T(8,128)S(1)} %fusion.16), slice={[0:16:2], [0:48:2], [0:128:2]} | slice | bytes 98304 | tf_op jit(solution)/shard_map/slice | solution.py:110
  39.5 1.3 collective-permute-start.5
  40.8 4.0 %collective-permute-start.4 = (f32[8,4,64]{2,0,1:T(8,128)S(1)}, f32[8,4,64]{2,0,1:T(8,128)S(1)}, u32[]{:S(2)}, u32[]{:S(2)}) collective-permute-start(f32[8,4,64]{2,0,1:T(8,128)S(1)} %get-tuple-element.45), channel_id=1, source_target_pairs={{0,16},{1,17},{2,18},{3,19},{4,20},{5,21},{6,22},{7,23},{8,24},{9,... | collective-permute-start | bytes 24584 | tf_op jit(solution)/shard_map/ppermute | solution.py:25
  44.9 0.8 collective-permute-done.4
  45.9 5.6 %collective-permute-start.7 = (f32[8,32,4]{2,0,1:T(8,128)S(1)}, f32[8,32,4]{2,0,1:T(8,128)S(1)}, u32[]{:S(2)}, u32[]{:S(2)}) collective-permute-start(f32[8,32,4]{2,0,1:T(8,128)S(1)} %get-tuple-element.42), channel_id=1, source_target_pairs={{1,0},{2,1},{3,2},{4,3},{5,4},{6,5},{7,6},{8,7},{9,8},{10,9},{11,1... | collective-permute-start | bytes 12296 | tf_op jit(solution)/shard_map/ppermute | solution.py:26
  51.8 2.8 %collective-permute-start.6 = (f32[8,32,4]{2,0,1:T(8,128)S(1)}, f32[8,32,4]{2,0,1:T(8,128)S(1)}, u32[]{:S(2)}, u32[]{:S(2)}) collective-permute-start(f32[8,32,4]{2,0,1:T(8,128)S(1)} %get-tuple-element.41), channel_id=1, source_target_pairs={{0,1},{1,2},{2,3},{3,4},{4,5},{5,6},{6,7},{7,8},{8,9},{9,10},{10,1... | collective-permute-start | bytes 12296 | tf_op jit(solution)/shard_map/ppermute | solution.py:25
  55.0 1.5 collective-permute-done.6
  57.7 1.4 slice.686
  59.1 1.3 collective-permute-start.9
  60.4 4.0 %collective-permute-start.8 = (f32[4,4,32]{2,0,1:T(4,128)S(1)}, f32[4,4,32]{2,0,1:T(4,128)S(1)}, u32[]{:S(2)}, u32[]{:S(2)}) collective-permute-start(f32[4,4,32]{2,0,1:T(4,128)S(1)} %get-tuple-element.55), channel_id=1, source_target_pairs={{0,16},{1,17},{2,18},{3,19},{4,20},{5,21},{6,22},{7,23},{8,24},{9,... | collective-permute-start | bytes 6152 | tf_op jit(solution)/shard_map/ppermute | solution.py:25
  64.5 0.7 collective-permute-done.8
  65.4 4.6 %collective-permute-start.11 = (f32[4,20,4]{2,0,1:T(4,128)S(1)}, f32[4,20,4]{2,0,1:T(4,128)S(1)}, u32[]{:S(2)}, u32[]{:S(2)}) collective-permute-start(f32[4,20,4]{2,0,1:T(4,128)S(1)} %get-tuple-element.52), channel_id=1, source_target_pairs={{1,0},{2,1},{3,2},{4,3},{5,4},{6,5},{7,6},{8,7},{9,8},{10,9},{11,1... | collective-permute-start | bytes 3848 | tf_op jit(solution)/shard_map/ppermute | solution.py:26
  70.3 3.7 %collective-permute-start.10 = (f32[4,20,4]{2,0,1:T(4,128)S(1)}, f32[4,20,4]{2,0,1:T(4,128)S(1)}, u32[]{:S(2)}, u32[]{:S(2)}) collective-permute-start(f32[4,20,4]{2,0,1:T(4,128)S(1)} %get-tuple-element.51), channel_id=1, source_target_pairs={{0,1},{1,2},{2,3},{3,4},{4,5},{5,6},{6,7},{7,8},{8,9},{9,10},{10,1... | collective-permute-start | bytes 3848 | tf_op jit(solution)/shard_map/ppermute | solution.py:25
  74.0 1.1 collective-permute-done.10
  76.0 0.6 slice.724
  76.7 1.3 collective-permute-start.13
  78.0 4.0 %collective-permute-start.12 = (f32[2,4,16]{2,0,1:T(2,128)S(1)}, f32[2,4,16]{2,0,1:T(2,128)S(1)}, u32[]{:S(2)}, u32[]{:S(2)}) collective-permute-start(f32[2,4,16]{2,0,1:T(2,128)S(1)} %get-tuple-element.63), channel_id=1, source_target_pairs={{0,16},{1,17},{2,18},{3,19},{4,20},{5,21},{6,22},{7,23},{8,24},{9,... | collective-permute-start | bytes 1544 | tf_op jit(solution)/shard_map/ppermute | solution.py:25
  82.9 3.6 %collective-permute-start.15 = (f32[2,14,4]{2,0,1:T(2,128)S(1)}, f32[2,14,4]{2,0,1:T(2,128)S(1)}, u32[]{:S(2)}, u32[]{:S(2)}) collective-permute-start(f32[2,14,4]{2,0,1:T(2,128)S(1)} %get-tuple-element.60), channel_id=1, source_target_pairs={{1,0},{2,1},{3,2},{4,3},{5,4},{6,5},{7,6},{8,7},{9,8},{10,9},{11,1... | collective-permute-start | bytes 1352 | tf_op jit(solution)/shard_map/ppermute | solution.py:26
  86.9 4.7 %collective-permute-start.14 = (f32[2,14,4]{2,0,1:T(2,128)S(1)}, f32[2,14,4]{2,0,1:T(2,128)S(1)}, u32[]{:S(2)}, u32[]{:S(2)}) collective-permute-start(f32[2,14,4]{2,0,1:T(2,128)S(1)} %get-tuple-element.59), channel_id=1, source_target_pairs={{0,1},{1,2},{2,3},{3,4},{4,5},{5,6},{6,7},{7,8},{8,9},{9,10},{10,1... | collective-permute-start | bytes 1352 | tf_op jit(solution)/shard_map/ppermute | solution.py:25
  91.7 0.6 collective-permute-done.14
  93.0 0.7 copy-done.9
  93.9 12.2 %scatter_fusion = f32[4,12,32]{2,0,1:T(4,128)S(1)} fusion(f32[4,12,32]{2,0,1:T(4,128)S(1)} %fusion.55, s32[192]{0:T(256)S(1)} %reshape.72, f32[192]{0:T(256)S(1)} %reshape.74), kind=kCustom, calls=%fused_computation | custom fusion | bytes 4608 | tf_op jit(solution)/shard_map/scatter | solution.py:111
  106.2 6.2 %scatter_fusion.1 = f32[12288]{0:T(1024)S(1)} fusion(f32[12288]{0:T(1024)S(1)} %reshape.64, s32[1536]{0:T(1024)S(1)} %reshape.78, f32[1536]{0:T(1024)S(1)} %reshape.80), kind=kCustom, calls=%fused_computation.1 | custom fusion | bytes 24576 | tf_op jit(solution)/shard_map/scatter | solution.py:111
  112.4 45.6 %scatter_fusion.2 = f32[98304]{0:T(1024)S(1)} fusion(f32[98304]{0:T(1024)S(1)} %bitcast.141, s32[12288]{0:T(1024)S(1)} %reshape.84, f32[12288]{0:T(1024)S(1)} %scatter_fusion.1), kind=kCustom, calls=%fused_computation.2 | custom fusion | bytes 196608
  158.0 0.7 convert_element_type.146
  (296 shorter events, 11.0 us)
Async XLA Ops:
  1.1 17.6 %collective-permute-start.1 = (f32[16,4,128]{2,1,0:T(4,128)S(1)}, f32[16,4,128]{2,1,0:T(4,128)S(1)}, u32[]{:S(2)}, u32[]{:S(2)}) collective-permute-start(f32[16,4,128]{2,1,0:T(4,128)S(1)} %get-tuple-element.36), channel_id=1, source_target_pairs={{16,0},{17,1},{18,2},{19,3},{20,4},{21,5},{22,6},{23,7},{24,8},{25... | collective-permute-start | bytes 98312 | tf_op jit(solution)/shard_map/ppermute | solution.py:26
  2.4 16.3 %collective-permute-start = (f32[16,4,128]{2,1,0:T(4,128)S(1)}, f32[16,4,128]{2,1,0:T(4,128)S(1)}, u32[]{:S(2)}, u32[]{:S(2)}) collective-permute-start(f32[16,4,128]{2,1,0:T(4,128)S(1)} %get-tuple-element.35), channel_id=1, source_target_pairs={{0,16},{1,17},{2,18},{3,19},{4,20},{5,21},{6,22},{7,23},{8,24},{9,... | collective-permute-start | bytes 98312 | tf_op jit(solution)/shard_map/ppermute | solution.py:25
  11.2 0.7 copy-start.13
  11.9 0.7 copy-start.14
  13.4 0.7 copy-start.12
  14.1 0.7 copy-start.11
  18.7 0.6 copy-start
  19.8 10.8 %collective-permute-start.3 = (f32[16,56,4]{2,1,0:T(8,128)S(1)}, f32[16,56,4]{2,1,0:T(8,128)S(1)}, u32[]{:S(2)}, u32[]{:S(2)}) collective-permute-start(f32[16,56,4]{2,1,0:T(8,128)S(1)} %get-tuple-element.32), channel_id=1, source_target_pairs={{1,0},{2,1},{3,2},{4,3},{5,4},{6,5},{7,6},{8,7},{9,8},{10,9},{11,1... | collective-permute-start | bytes 43016 | tf_op jit(solution)/shard_map/ppermute | solution.py:26
  24.7 8.7 %collective-permute-start.2 = (f32[16,56,4]{2,1,0:T(8,128)S(1)}, f32[16,56,4]{2,1,0:T(8,128)S(1)}, u32[]{:S(2)}, u32[]{:S(2)}) collective-permute-start(f32[16,56,4]{2,1,0:T(8,128)S(1)} %get-tuple-element.31), channel_id=1, source_target_pairs={{0,1},{1,2},{2,3},{3,4},{4,5},{5,6},{6,7},{7,8},{8,9},{9,10},{10,1... | collective-permute-start | bytes 43016 | tf_op jit(solution)/shard_map/ppermute | solution.py:25
  30.6 2.9 %copy-start.1 = (f32[16,4,128]{2,1,0:T(4,128)S(1)}, f32[16,4,128]{2,1,0:T(4,128)}, u32[]{:S(2)}) copy-start(f32[16,4,128]{2,1,0:T(4,128)} %copy-done) | copy-start | bytes 98308
  39.5 5.3 %copy-start.2 = (f32[12,1,24]{2,1,0:T(1,128)S(1)}, f32[12,1,24]{2,1,0:T(1,128)}, u32[]{:S(2)}) copy-start(f32[12,1,24]{2,1,0:T(1,128)} %stack.139) | copy-start | bytes 3460
  39.5 5.3 %copy-start.3 = (f32[12,1,24]{2,1,0:T(1,128)S(1)}, f32[12,1,24]{2,1,0:T(1,128)}, u32[]{:S(2)}) copy-start(f32[12,1,24]{2,1,0:T(1,128)} %copy.81) | copy-start | bytes 3460
  39.5 5.3 %collective-permute-start.5 = (f32[8,4,64]{2,0,1:T(8,128)S(1)}, f32[8,4,64]{2,0,1:T(8,128)S(1)}, u32[]{:S(2)}, u32[]{:S(2)}) collective-permute-start(f32[8,4,64]{2,0,1:T(8,128)S(1)} %get-tuple-element.46), channel_id=1, source_target_pairs={{16,0},{17,1},{18,2},{19,3},{20,4},{21,5},{22,6},{23,7},{24,8},{25... | collective-permute-start | bytes 24584 | tf_op jit(solution)/shard_map/ppermute | solution.py:26
  40.8 4.8 %collective-permute-start.4 = (f32[8,4,64]{2,0,1:T(8,128)S(1)}, f32[8,4,64]{2,0,1:T(8,128)S(1)}, u32[]{:S(2)}, u32[]{:S(2)}) collective-permute-start(f32[8,4,64]{2,0,1:T(8,128)S(1)} %get-tuple-element.45), channel_id=1, source_target_pairs={{0,16},{1,17},{2,18},{3,19},{4,20},{5,21},{6,22},{7,23},{8,24},{9,... | collective-permute-start | bytes 24584 | tf_op jit(solution)/shard_map/ppermute | solution.py:25
  45.7 5.8 %copy-start.6 = (f32[4,1,8]{2,0,1:T(4,128)S(1)}, f32[4,1,8]{2,0,1:T(4,128)}, u32[]{:S(2)}) copy-start(f32[4,1,8]{2,0,1:T(4,128)} %get-tuple-element.19) | copy-start | bytes 388
  45.9 5.7 %copy-start.5 = (f32[4,1,8]{2,0,1:T(4,128)S(1)}, f32[4,1,8]{2,0,1:T(4,128)}, u32[]{:S(2)}) copy-start(f32[4,1,8]{2,0,1:T(4,128)} %fusion.161) | copy-start | bytes 388
  45.9 9.1 %collective-permute-start.7 = (f32[8,32,4]{2,0,1:T(8,128)S(1)}, f32[8,32,4]{2,0,1:T(8,128)S(1)}, u32[]{:S(2)}, u32[]{:S(2)}) collective-permute-start(f32[8,32,4]{2,0,1:T(8,128)S(1)} %get-tuple-element.42), channel_id=1, source_target_pairs={{1,0},{2,1},{3,2},{4,3},{5,4},{6,5},{7,6},{8,7},{9,8},{10,9},{11,1... | collective-permute-start | bytes 12296 | tf_op jit(solution)/shard_map/ppermute | solution.py:26
  51.8 4.7 %collective-permute-start.6 = (f32[8,32,4]{2,0,1:T(8,128)S(1)}, f32[8,32,4]{2,0,1:T(8,128)S(1)}, u32[]{:S(2)}, u32[]{:S(2)}) collective-permute-start(f32[8,32,4]{2,0,1:T(8,128)S(1)} %get-tuple-element.41), channel_id=1, source_target_pairs={{0,1},{1,2},{2,3},{3,4},{4,5},{5,6},{6,7},{7,8},{8,9},{9,10},{10,1... | collective-permute-start | bytes 12296 | tf_op jit(solution)/shard_map/ppermute | solution.py:25
  59.1 5.3 %collective-permute-start.9 = (f32[4,4,32]{2,0,1:T(4,128)S(1)}, f32[4,4,32]{2,0,1:T(4,128)S(1)}, u32[]{:S(2)}, u32[]{:S(2)}) collective-permute-start(f32[4,4,32]{2,0,1:T(4,128)S(1)} %get-tuple-element.56), channel_id=1, source_target_pairs={{16,0},{17,1},{18,2},{19,3},{20,4},{21,5},{22,6},{23,7},{24,8},{25... | collective-permute-start | bytes 6152 | tf_op jit(solution)/shard_map/ppermute | solution.py:26
  60.4 4.8 %collective-permute-start.8 = (f32[4,4,32]{2,0,1:T(4,128)S(1)}, f32[4,4,32]{2,0,1:T(4,128)S(1)}, u32[]{:S(2)}, u32[]{:S(2)}) collective-permute-start(f32[4,4,32]{2,0,1:T(4,128)S(1)} %get-tuple-element.55), channel_id=1, source_target_pairs={{0,16},{1,17},{2,18},{3,19},{4,20},{5,21},{6,22},{7,23},{8,24},{9,... | collective-permute-start | bytes 6152 | tf_op jit(solution)/shard_map/ppermute | solution.py:25
  65.4 4.7 %copy-start.8 = (f32[2,1,4]{2,0,1:T(2,128)S(1)}, f32[2,1,4]{2,0,1:T(2,128)}, u32[]{:S(2)}) copy-start(f32[2,1,4]{2,0,1:T(2,128)} %get-tuple-element.13) | copy-start | bytes 100
  65.4 4.7 %copy-start.7 = (f32[2,1,4]{2,0,1:T(2,128)S(1)}, f32[2,1,4]{2,0,1:T(2,128)}, u32[]{:S(2)}) copy-start(f32[2,1,4]{2,0,1:T(2,128)} %fusion.174) | copy-start | bytes 100
  65.4 8.6 %collective-permute-start.11 = (f32[4,20,4]{2,0,1:T(4,128)S(1)}, f32[4,20,4]{2,0,1:T(4,128)S(1)}, u32[]{:S(2)}, u32[]{:S(2)}) collective-permute-start(f32[4,20,4]{2,0,1:T(4,128)S(1)} %get-tuple-element.52), channel_id=1, source_target_pairs={{1,0},{2,1},{3,2},{4,3},{5,4},{6,5},{7,6},{8,7},{9,8},{10,9},{11,1... | collective-permute-start | bytes 3848 | tf_op jit(solution)/shard_map/ppermute | solution.py:26
  70.3 4.8 %collective-permute-start.10 = (f32[4,20,4]{2,0,1:T(4,128)S(1)}, f32[4,20,4]{2,0,1:T(4,128)S(1)}, u32[]{:S(2)}, u32[]{:S(2)}) collective-permute-start(f32[4,20,4]{2,0,1:T(4,128)S(1)} %get-tuple-element.51), channel_id=1, source_target_pairs={{0,1},{1,2},{2,3},{3,4},{4,5},{5,6},{6,7},{7,8},{8,9},{9,10},{10,1... | collective-permute-start | bytes 3848 | tf_op jit(solution)/shard_map/ppermute | solution.py:25
  76.7 5.3 %copy-start.4 = (f32[7,1,14]{2,0,1:T(8,128)S(1)}, f32[7,1,14]{2,0,1:T(8,128)}, u32[]{:S(2)}) copy-start(f32[7,1,14]{2,0,1:T(8,128)} %fusion.150) | copy-start | bytes 1180
  76.7 5.6 %collective-permute-start.13 = (f32[2,4,16]{2,0,1:T(2,128)S(1)}, f32[2,4,16]{2,0,1:T(2,128)S(1)}, u32[]{:S(2)}, u32[]{:S(2)}) collective-permute-start(f32[2,4,16]{2,0,1:T(2,128)S(1)} %get-tuple-element.64), channel_id=1, source_target_pairs={{16,0},{17,1},{18,2},{19,3},{20,4},{21,5},{22,6},{23,7},{24,8},{25... | collective-permute-start | bytes 1544 | tf_op jit(solution)/shard_map/ppermute | solution.py:26
  78.0 4.7 %collective-permute-start.12 = (f32[2,4,16]{2,0,1:T(2,128)S(1)}, f32[2,4,16]{2,0,1:T(2,128)S(1)}, u32[]{:S(2)}, u32[]{:S(2)}) collective-permute-start(f32[2,4,16]{2,0,1:T(2,128)S(1)} %get-tuple-element.63), channel_id=1, source_target_pairs={{0,16},{1,17},{2,18},{3,19},{4,20},{5,21},{6,22},{7,23},{8,24},{9,... | collective-permute-start | bytes 1544 | tf_op jit(solution)/shard_map/ppermute | solution.py:25
  82.9 8.9 %collective-permute-start.15 = (f32[2,14,4]{2,0,1:T(2,128)S(1)}, f32[2,14,4]{2,0,1:T(2,128)S(1)}, u32[]{:S(2)}, u32[]{:S(2)}) collective-permute-start(f32[2,14,4]{2,0,1:T(2,128)S(1)} %get-tuple-element.60), channel_id=1, source_target_pairs={{1,0},{2,1},{3,2},{4,3},{5,4},{6,5},{7,6},{8,7},{9,8},{10,9},{11,1... | collective-permute-start | bytes 1352 | tf_op jit(solution)/shard_map/ppermute | solution.py:26
  86.9 5.4 %collective-permute-start.14 = (f32[2,14,4]{2,0,1:T(2,128)S(1)}, f32[2,14,4]{2,0,1:T(2,128)S(1)}, u32[]{:S(2)}, u32[]{:S(2)}) collective-permute-start(f32[2,14,4]{2,0,1:T(2,128)S(1)} %get-tuple-element.59), channel_id=1, source_target_pairs={{0,1},{1,2},{2,3},{3,4},{4,5},{5,6},{6,7},{7,8},{8,9},{9,10},{10,1... | collective-permute-start | bytes 1352 | tf_op jit(solution)/shard_map/ppermute | solution.py:25
  93.0 0.7 copy-start.9
  93.0 0.7 copy-start.10
where the time goes:
time: 161 us; the launch traced here: 159 us
  local copies, waits for them, and re-layouts  81.6 us (51%)
  starting transfers between devices  52.6 us (33%)
  waiting for transfers between devices  10.9 us (7%)
  other arithmetic  7.8 us (5%)
  matrix products  3.93 us (2%)
  between operations  1.79 us (1%)
    unnamed x35, local copies, waits for them, and re-layouts  49.3 us
    ppermute x8, starting transfers between devices, padded(): before = lax.ppermute(last, axis, up)  30.4 us
    ppermute x8, starting transfers between devices, padded(): after = lax.ppermute(initial, axis, down)  22.2 us
    scatter x4, local copies, waits for them, and re-layouts, decompose(): subband = subband.at[::2, ::2, ::2].set(coarser)  18.5 us
    ppermute x8, waiting for transfers between devices, padded(): before = lax.ppermute(last, axis, up)  8 us
    slice x3, local copies, waits for them, and re-layouts, decompose(): coarser = decompose(subband[::2, ::2, ::2], level_index + 1)  5.59 us
    another operation x27, other arithmetic, lift_local(): return jnp.stack([even_part, odd_part], along + 1).reshape(subband.shape)  4.12 us
  transfers between devices with their start and end apart: 16, of which 9 were waited for; matrix products, arithmetic and copies ran while one was open for 8% of the time, Pallas kernels for 0%

commit v1 on v0

v1 whole, which is shorter than its diff:
```python
import numpy as np
import jax
import jax.numpy as jnp
from jax import lax
from jax.experimental import pallas as pl
from jax.experimental.pallas import tpu as pltpu
from jax.sharding import PartitionSpec as P

LEVELS = 4
LANES = 128

LIFT_ALPHA = -1.586134342059924
LIFT_BETA = -0.052980118572961
LIFT_GAMMA = 0.882911075530934
LIFT_DELTA = 0.443506852043971
LIFT_KAPPA = 1.230174104914001


def lift_matrix(m):
    e, o = m[0::2], m[1::2]
    after = lambda v: np.concatenate([v[1:], v[-1:]])
    before = lambda v: np.concatenate([v[:1], v[:-1]])
    o = o + LIFT_ALPHA * (e + after(e))
    e = e + LIFT_BETA * (before(o) + o)
    o = o + LIFT_GAMMA * (e + after(e))
    e = e + LIFT_DELTA * (before(o) + o)
    return np.stack([e / LIFT_KAPPA, o * (LIFT_KAPPA / 2.0)], 1).reshape(m.shape)


def operators(length):
    low, ops = np.eye(length), []
    for _ in range(LEVELS):
        full = lift_matrix(low)
        ops.append(full)
        low = full[0::2]
    return ops


def factor(block):
    rest, us, vs = block.copy(), [], []
    top = np.abs(block).max()
    while top > 0 and np.abs(rest).max() > 1e-12 * top:
        i, j = np.unravel_index(np.argmax(np.abs(rest)), rest.shape)
        u, v = rest[:, j] / rest[i, j], rest[i].copy()
        rest = rest - u[:, None] * v[None]
        us.append(u)
        vs.append(v)
    rows, cols = block.shape
    return (
        np.stack(us, 1) if us else np.zeros((rows, 0)),
        np.stack(vs, 0) if vs else np.zeros((0, cols)),
    )


class Plan:
    def __init__(self, count, block):
        assert count == 1 or count % 2 == 0
        long = block >= 2 * sum(4 << l for l in range(LEVELS))
        kinds = min(count, 4) if long else count
        self.count, self.block, self.kinds = count, block, kinds
        ops = operators(kinds * block)
        size = [block >> l for l in range(LEVELS)]
        cut = lambda l, q, p: ops[l][q * size[l] : (q + 1) * size[l], p * block : (p + 1) * block]
        self.own = [[cut(l, p, p) for l in range(LEVELS)] for p in range(kinds)]
        moves = [lambda p: p ^ 1, lambda p: ((p + 1) ^ 1) - 1]
        for hop in range(2, kinds):
            moves += [lambda p, hop=hop: p + hop, lambda p, hop=hop: p - hop]
        self.perms, self.rank, self.u, self.v = [], [], [], []
        for move in moves:
            pairs = [(p, move(p)) for p in range(kinds) if 0 <= move(p) < kinds]
            parts = {pq: [factor(cut(l, pq[1], pq[0])) for l in range(LEVELS)] for pq in pairs}
            rank = [max([f[l][0].shape[1] for f in parts.values()] + [0]) for l in range(LEVELS)]
            if not sum(rank):
                continue
            assert max(rank) <= 8
            u = [[np.zeros((size[l], rank[l])) for l in range(LEVELS)] for _ in range(kinds)]
            v = [[np.zeros((rank[l], block)) for l in range(LEVELS)] for _ in range(kinds)]
            for (p, q), fs in parts.items():
                for l, (fu, fv) in enumerate(fs):
                    u[q][l][:, : fu.shape[1]] = fu
                    v[p][l][: fv.shape[0]] = fv
            self.perms.append([(p, move(p)) for p in range(count) if 0 <= move(p) < count])
            self.rank.append(rank)
            self.u.append(u)
            self.v.append(v)

    def kind(self, axis):
        p = lax.axis_index(axis)
        if self.kinds == self.count:
            return p
        return jnp.where(p == 0, 0, jnp.where(p == self.count - 1, 3, 2 - lax.rem(p, 2)))


def up(n, m):
    return -(-n // m) * m


def split_np(m):
    hi = m.astype(jnp.bfloat16)
    return hi, (m - hi.astype(np.float64)).astype(jnp.bfloat16)


def split(x):
    hi = x.astype(jnp.bfloat16)
    return hi, (x - hi.astype(jnp.float32)).astype(jnp.bfloat16)


def lift_planes(planes):
    e, o = planes[0::2], planes[1::2]
    n = len(e)
    after = lambda v, i: v[min(i + 1, n - 1)]
    before = lambda v, i: v[max(i - 1, 0)]
    o = [o[i] + LIFT_ALPHA * (e[i] + after(e, i)) for i in range(n)]
    e = [e[i] + LIFT_BETA * (before(o, i) + o[i]) for i in range(n)]
    o = [o[i] + LIFT_GAMMA * (e[i] + after(e, i)) for i in range(n)]
    e = [e[i] + LIFT_DELTA * (before(o, i) + o[i]) for i in range(n)]
    out = []
    for i in range(n):
        out += [e[i] * (1.0 / LIFT_KAPPA), o[i] * (LIFT_KAPPA / 2.0)]
    return out


def mm(a, b, dims):
    return lax.dot_general(a, b, (dims, ((), ())), preferred_element_type=jnp.float32)


NN, NT, TN = ((1,), (0,)), ((1,), (1,)), ((0,), (0,))
VMEM = pl.BlockSpec(memory_space=pltpu.VMEM)


def call(kernel, outs, args, scratch=(), flops=0, specs=None):
    moved = sum(int(np.prod(a.shape)) * a.dtype.itemsize for a in list(args) + list(outs))
    many = len(outs) > 1
    return pl.pallas_call(
        kernel,
        out_shape=tuple(outs) if many else outs[0],
        in_specs=specs or [VMEM] * len(args),
        out_specs=(VMEM,) * len(outs) if many else VMEM,
        scratch_shapes=list(scratch),
        cost_estimate=pl.CostEstimate(flops=flops, bytes_accessed=moved, transcendentals=0),
    )(*args)


def body_of(ny, nx):
    def body(quantized, scales):
        nz, rows, cols = quantized.shape
        assert scales.shape == (1, nz, rows) and cols == LANES
        assert nz % (1 << LEVELS) == 0 and rows % 8 == 0 and (nz * rows) % LANES == 0
        f32, bf16 = jnp.float32, jnp.bfloat16
        yplan, xplan = Plan(ny, rows), Plan(nx, cols)
        ey, ex = range(len(yplan.perms)), range(len(xplan.perms))
        lv = range(LEVELS)
        planes = [nz >> l for l in lv]
        height = [rows >> l for l in lv]
        base = [sum(planes[i] * height[i] for i in range(l)) for l in range(LEVELS + 1)]
        total = up(base[-1], LANES)
        chunks, chunks0 = total // LANES, base[1] // LANES

        yoff = [sum(up(height[i], 8) for i in range(l)) for l in range(LEVELS + 1)]
        yown = np.zeros((yplan.kinds, yoff[-1], rows), np.float32)
        ucoef = np.zeros((yplan.kinds, yoff[-1], LANES), np.float32)
        voff, at = {}, 0
        for l in lv:
            for e in ey:
                voff[e, l] = at
                at += yplan.rank[e][l]
        vmat = np.zeros((yplan.kinds, up(at, 8), rows), np.float32)
        for p in range(yplan.kinds):
            for l in lv:
                yown[p, yoff[l] : yoff[l] + height[l]] = yplan.own[p][l]
                for e in ey:
                    r = yplan.rank[e][l]
                    vmat[p, voff[e, l] : voff[e, l] + r] = yplan.v[e][p][l]
                    ucoef[p, yoff[l] : yoff[l] + height[l], 8 * e : 8 * e + r] = yplan.u[e][p][l]
        mbase = [[sum(planes[i] * yplan.rank[e][i] for i in range(l)) for l in range(LEVELS + 1)] for e in ey]
        mrows = [up(mbase[e][-1], 8) for e in ey]

        ne = len(xplan.perms)
        r0 = max([xplan.rank[e][0] for e in ex] + [1])
        xrows0 = up(r0 * chunks0, 8)
        xmsg = xrows0 + 8 * (chunks - chunks0)
        k0 = up(ne * r0, 8)
        s0 = np.zeros((xplan.kinds, 2 * k0, LANES), np.float32)
        s1 = np.zeros((xplan.kinds, 2 * ne * (LEVELS - 1) * 8, LANES), np.float32)
        half1 = ne * (LEVELS - 1) * 8
        kr = up(3 * k0, 16)
        ur0 = np.zeros((xplan.kinds, kr, LANES), np.float32)
        k1 = up(ne * 8, 16)
        ur1 = np.zeros((xplan.kinds, LEVELS - 1, 3 * k1, LANES), np.float32)
        xown = np.zeros((xplan.kinds, LEVELS, 3, LANES, LANES), np.float32)
        f = lambda m: np.asarray(m, np.float32)
        for p in range(xplan.kinds):
            for l in lv:
                step = 1 << l
                placed = np.zeros((LANES, LANES))
                placed[:, ::step] = xplan.own[p][l].T
                hi, lo = split_np(placed)
                xown[p, l] = np.stack([f(hi), f(hi), f(lo)])
                for e in ex:
                    r = xplan.rank[e][l]
                    vh, vl = split_np(xplan.v[e][p][l])
                    um = np.zeros((r, LANES))
                    um[:, ::step] = xplan.u[e][p][l].T
                    uh, ul = split_np(um)
                    if l == 0:
                        s0[p, e * r0 : e * r0 + r] = f(vh)
                        s0[p, k0 + e * r0 : k0 + e * r0 + r] = f(vl)
                        for j, w in enumerate((uh, uh, ul)):
                            ur0[p, j * k0 + e * r0 : j * k0 + e * r0 + r] = f(w)
                    else:
                        o = (e * (LEVELS - 1) + l - 1) * 8
                        s1[p, o : o + r] = f(vh)
                        s1[p, half1 + o : half1 + o + r] = f(vl)
                        for j, w in enumerate((uh, uh, ul)):
                            ur1[p, l - 1, j * k1 + e * 8 : j * k1 + e * 8 + r] = f(w)
        tab = lambda m, t: jnp.asarray(m.astype(t))

        def scaled(mat, s, q):
            hi, lo = split(mat * s)
            out = mm(jnp.concatenate([hi, lo], 0), q, NN)
            return out[: mat.shape[0]] + out[mat.shape[0] :]

        def k_send_y(q_ref, s_ref, v_ref, *outs):
            v = v_ref[yplan.kind("grp")]
            part = [scaled(v, s_ref[0, z : z + 1, :], q_ref[z]) for z in range(nz)]
            for l in lv:
                part = lift_planes(part)
                for e in ey:
                    r, o = yplan.rank[e][l], voff[e, l]
                    for k in range(planes[l]):
                        if r:
                            outs[e][mbase[e][l] + k * r : mbase[e][l] + (k + 1) * r, :] = part[k][o : o + r]
                part = part[0::2]
            for e in ey:
                if mrows[e] > mbase[e][-1]:
                    outs[e][mbase[e][-1] :, :] = jnp.zeros((mrows[e] - mbase[e][-1], LANES), f32)

        def k_own_yz(q_ref, s_ref, y_ref, d_ref, t_ref):
            y = y_ref[yplan.kind("grp")]
            for z in range(nz):
                t_ref[z] = scaled(y, s_ref[0, z : z + 1, :], q_ref[z])
            for l in lv:
                for t in range(yoff[l], yoff[l + 1], 8):
                    part = [t_ref[z, t : t + 8, :] for z in range(nz)]
                    for _ in range(l):
                        part = lift_planes(part)[0::2]
                    part = lift_planes(part)
                    n = min(8, yoff[l] + height[l] - t)
                    for k in range(planes[l]):
                        o = base[l] + k * height[l] + t - yoff[l]
                        d_ref[o : o + n, :] = part[k][:n]
            if total > base[-1]:
                d_ref[base[-1] :, :] = jnp.zeros((total - base[-1], LANES), f32)

        def k_send_x(d_ref, *refs):
            ms, (u_ref, s0_ref, s1_ref) = refs[: len(ey)], refs[len(ey) : len(ey) + 3]
            o_ref, outs = refs[len(ey) + 3], refs[len(ey) + 4 :]
            p = yplan.kind("grp")
            for l in lv:
                for t in range(0, height[l], 8):
                    n = min(8, height[l] - t)
                    u = u_ref[p, yoff[l] + t : yoff[l] + t + n, :]
                    cs = {(e, i): u[:, 8 * e + i : 8 * e + i + 1] for e in ey for i in range(yplan.rank[e][l])}
                    cs = {key: jnp.broadcast_to(c, (n, LANES)) for key, c in cs.items()}
                    for k in range(planes[l]):
                        o = base[l] + k * height[l] + t
                        acc = d_ref[o : o + n, :]
                        for (e, i), c in cs.items():
                            row = mbase[e][l] + k * yplan.rank[e][l] + i
                            acc = acc + c * ms[e][row : row + 1, :]
                        o_ref[o : o + n, :] = acc
            if total > base[-1]:
                o_ref[base[-1] :, :] = jnp.zeros((total - base[-1], LANES), f32)
            px = xplan.kind("tile")
            a0, a1 = s0_ref[px], s1_ref[px]
            a0, a1 = jnp.concatenate([a0, a0], 1), jnp.concatenate([a1, a1], 1)
            lane = lax.broadcasted_iota(jnp.int32, (8, LANES), 1)
            for c in range(chunks):
                d = jnp.concatenate(split(o_ref[c * LANES : (c + 1) * LANES, :]), 1)
                if c < chunks0:
                    m = mm(a0, d, NT)
                    m = m[:k0] + m[k0:]
                    for e in ex:
                        outs[e][r0 * c : r0 * (c + 1), :] = m[e * r0 : (e + 1) * r0]
                else:
                    m = mm(a1, d, NT)
                    m = m[:half1] + m[half1:]
                    for e in ex:
                        o = e * (LEVELS - 1) * 8
                        val = m[o : o + 8]
                        for l in range(2, LEVELS):
                            val = jnp.where(lane + c * LANES >= base[l], m[o + (l - 1) * 8 : o + l * 8], val)
                        w = xrows0 + 8 * (c - chunks0)
                        outs[e][w : w + 8, :] = val
            for e in ex:
                if xrows0 > r0 * chunks0:
                    outs[e][r0 * chunks0 : xrows0, :] = jnp.zeros((xrows0 - r0 * chunks0, LANES), f32)

        def k_own_x(d_ref, x_ref, o_ref, x_vmem, sem):
            copy = pltpu.make_async_copy(x_ref.at[xplan.kind("tile")], x_vmem, sem)
            copy.start()
            copy.wait()
            for l in lv:
                end = base[l + 1] if l + 1 < LEVELS else total
                hi, lo = split(d_ref[base[l] : end, :])
                o_ref[base[l] : end, :] = mm(jnp.concatenate([hi, lo, hi], 1), x_vmem[l], NN)

        def k_join(f_ref, *refs):
            ms, (u0_ref, u1_ref, out_ref, acc, low) = refs[: len(ex)], refs[len(ex) :]
            px = xplan.kind("tile")
            u0 = u0_ref[px]
            for c in range(chunks0):
                rows_in = [ms[e][r0 * c : r0 * (c + 1), :] for e in ex]
                if k0 > ne * r0:
                    rows_in.append(jnp.zeros((k0 - ne * r0, LANES), f32))
                m = jnp.concatenate(rows_in, 0)
                hi, lo = split(m)
                parts = [hi.astype(f32), lo.astype(f32), hi.astype(f32)]
                if kr > 3 * k0:
                    parts.append(jnp.zeros((kr - 3 * k0, LANES), f32))
                lhs = jnp.concatenate(parts, 0).astype(bf16)
                acc[c * LANES : (c + 1) * LANES, :] = f_ref[c * LANES : (c + 1) * LANES, :] + mm(lhs, u0, TN)
            for c in range(chunks0, chunks):
                w = xrows0 + 8 * (c - chunks0)
                rows_in = [ms[e][w : w + 8, :] for e in ex]
                if k1 > 8 * ne:
                    rows_in.append(jnp.zeros((k1 - 8 * ne, LANES), f32))
                hi, lo = split(jnp.concatenate(rows_in, 0))
                lhs = jnp.concatenate([hi, lo, hi], 0)
                for l in range(1, LEVELS):
                    a = max(base[l], c * LANES)
                    end = base[l + 1] if l + 1 < LEVELS else total
                    b = min(end, (c + 1) * LANES)
                    if a < b:
                        m = mm(lhs, u1_ref[px, l - 1], TN)
                        low[a - base[1] : b - base[1], :] = f_ref[a:b, :] + m[a - c * LANES : b - c * LANES]
            for l in range(1, LEVELS):
                step, h = 1 << l, height[l]
                lane = lax.broadcasted_iota(jnp.int32, (h, LANES), 1)
                for k in range(planes[l]):
                    o = base[l] - base[1] + k * h
                    at = pl.ds(k * step * rows, h, stride=step)
                    acc[at, :] = jnp.where(lane % step == 0, low[o : o + h, :], acc[at, :])
            for z in range(nz):
                out_ref[z] = acc[z * rows : (z + 1) * rows, :].astype(bf16)

        shape = jax.ShapeDtypeStruct
        sent = call(
            k_send_y,
            [shape((mrows[e], LANES), f32) for e in ey],
            [quantized, scales, tab(vmat, f32)],
            flops=1000000,
        )
        sent = sent if isinstance(sent, (tuple, list)) else [sent]
        got = [lax.ppermute(sent[e], "grp", yplan.perms[e]) for e in ey]
        d = call(
            k_own_yz,
            [shape((total, LANES), f32)],
            [quantized, scales, tab(yown, f32)],
            [pltpu.VMEM((nz, yoff[-1], LANES), f32)],
            flops=100000000,
        )
        d, *sent = call(
            k_send_x,
            [shape((total, LANES), f32)] + [shape((xmsg, LANES), f32) for e in ex],
            [d, *got, tab(ucoef, f32), tab(s0, bf16), tab(s1, bf16)],
            flops=10000000,
        )
        got = [lax.ppermute(sent[e], "tile", xplan.perms[e]) for e in ex]
        xtab = tab(xown.reshape(xplan.kinds, LEVELS, 3 * LANES, LANES), bf16)
        full = call(
            k_own_x,
            [shape((total, LANES), f32)],
            [d, xtab],
            [pltpu.VMEM((LEVELS, 3 * LANES, LANES), bf16), pltpu.SemaphoreType.DMA],
            flops=100000000,
            specs=[VMEM, pl.BlockSpec(memory_space=pl.ANY)],
        )
        return call(
            k_join,
            [shape(quantized.shape, bf16)],
            [full, *got, tab(ur0, bf16), tab(ur1, bf16)],
            [pltpu.VMEM((base[1], LANES), f32), pltpu.VMEM((total - base[1], LANES), f32)],
            flops=10000000,
        )

    return body


def solution(mesh):
    return jax.shard_map(
        body_of(mesh.shape["grp"], mesh.shape["tile"]),
        mesh=mesh,
        in_specs=(P(None, "grp", "tile"), P("tile", None, "grp")),
        out_specs=P(None, "grp", "tile"),
        check_vma=False,
    )
```

time: 161 us -> 20.1 us (0.12)
  the two profiles are of different devices: /device:TPU:21 before, /device:TPU:1 now
where the time goes in v1:
time: 20.1 us; the launch traced here: 19.8 us
  Pallas kernels  11.5 us (57%)
  starting transfers between devices  6.44 us (32%)
  local copies, waits for them, and re-layouts  1.79 us (9%)
    pallas_call x5, Pallas kernels, call(): pl.pallas_call(kernel, out_shape=tuple(outs) if many else outs[0], in_spe...  11.5 us
    ppermute x2, starting transfers between devices, body(): got = [lax.ppermute(sent[e], 'tile', xplan.perms[e]) for e in ex]  4.42 us
    ppermute x1, starting transfers between devices, body(): got = [lax.ppermute(sent[e], 'grp', yplan.perms[e]) for e in ey]  2.03 us
    unnamed x6, local copies, waits for them, and re-layouts  1.79 us
  transfers between devices with their start and end apart: 3, of which 0 were waited for; matrix products, arithmetic and copies ran while one was open for 0% of the time, Pallas kernels for 28%

profile of v1, /device:TPU:1, one launch (start us, length us, event | category | flops | bytes accessed | tf_op | source)
XLA Modules:
  0.0 19.8 jit_solution(16189323766696276994)
XLA Ops:
  0.0 1.8 %shard_map.101 = f32[80,128]{1,0:T(8,128)} custom-call(bf16[16,48,128]{2,1,0:T(8,128)(2,1)} %q_ref.3, f32[1,16,48]{2,1,0:T(8,128)} %s_ref.3, f32[2,16,48]{2,1,0:T(8,128)} %constant.16.clone.v_ref), custom_call_target="tpu_custom_call" | custom-call | flops 1000000 | bytes 246784 | tf_op jit(solution)/shard_map/pallas_call | solution.py:134
  1.8 2.0 %collective-permute-start = (f32[80,128]{1,0:T(8,128)}, f32[80,128]{1,0:T(8,128)S(1)}, u32[]{:S(2)}, u32[]{:S(2)}) collective-permute-start(f32[80,128]{1,0:T(8,128)} %shard_map.101), channel_id=1, source_target_pairs={{0,16},{16,0},{1,17},{17,1},{2,18},{18,2},{3,19},{19,3},{4,20},{20... | collective-permute-start | bytes 122888 | tf_op jit(solution)/shard_map/ppermute | solution.py:355
  3.8 2.3 %shard_map.100.d_ref = f32[1024,128]{1,0:T(8,128)} custom-call(bf16[16,48,128]{2,1,0:T(8,128)(2,1)} %q_ref.3, f32[1,16,48]{2,1,0:T(8,128)} %s_ref.3, f32[2,96,48]{2,1,0:T(8,128)} %constant.17.clone.y_ref), custom_call_target="tpu_custom_call" | custom-call | flops 100000000 | bytes 760832 | tf_op jit(solution)/shard_map/pallas_call | solution.py:134
  6.1 0.0 collective-permute-done.refs_0_
  6.1 0.0 copy-start
  6.1 0.6 %copy-done = f32[80,128]{1,0:T(8,128)} copy-done((f32[80,128]{1,0:T(8,128)}, f32[80,128]{1,0:T(8,128)S(1)}, u32[]{:S(2)}) %copy-start) | copy-done | bytes 40984
  6.7 2.1 %shard_map.102 = (f32[1024,128]{1,0:T(8,128)}, f32[32,128]{1,0:T(8,128)}, f32[32,128]{1,0:T(8,128)}) custom-call(f32[1024,128]{1,0:T(8,128)} %shard_map.100.d_ref, f32[80,128]{1,0:T(8,128)} %copy-done, f32[2,96,128]{2,1,0:T(8,128)} %constant.18.clone.refs_1_, bf16[4,16,128]{2,1,0:T(8,128)(2,1)} %constant.19.clone.refs_2_, ...), custom_call_target="tpu_custom_call" | custom-call | flops 10000000 | bytes 1335296 | tf_op jit(solution)/shard_map/pallas_call | solution.py:134
  8.9 1.0 %collective-permute-start.1 = (f32[32,128]{1,0:T(8,128)}, f32[32,128]{1,0:T(8,128)S(1)}, u32[]{:S(2)}, u32[]{:S(2)}) collective-permute-start(f32[32,128]{1,0:T(8,128)} %get-tuple-element.9), channel_id=1, source_target_pairs={{0,1},{1,0},{2,3},{3,2},{4,5},{5,4},{6,7},{7,6},{8,9},{9,8},{10,11... | collective-permute-start | bytes 49160 | tf_op jit(solution)/shard_map/ppermute | solution.py:369
  9.8 3.5 %collective-permute-start.2 = (f32[32,128]{1,0:T(8,128)}, f32[32,128]{1,0:T(8,128)S(1)}, u32[]{:S(2)}, u32[]{:S(2)}) collective-permute-start(f32[32,128]{1,0:T(8,128)} %get-tuple-element.10), channel_id=1, source_target_pairs={{1,2},{2,1},{3,4},{4,3},{5,6},{6,5},{7,8},{8,7},{9,10},{10,9},{11,... | collective-permute-start | bytes 49160 | tf_op jit(solution)/shard_map/ppermute | solution.py:369
  13.3 3.2 %shard_map.103.f_ref = f32[1024,128]{1,0:T(8,128)} custom-call(f32[1024,128]{1,0:T(8,128)} %get-tuple-element.8.d_ref, bf16[4,4,384,128]{3,2,1,0:T(8,128)(2,1)} %constant.21.clone.x_ref), custom_call_target="tpu_custom_call" | custom-call | flops 100000000 | bytes 2621440 | tf_op jit(solution)/shard_map/pallas_call | solution.py:134
  16.5 0.0 collective-permute-done.1.refs_0_
  16.5 0.0 copy-start.1
  16.5 0.0 collective-permute-done.2.refs_1_
  16.5 0.6 %copy-done.1 = f32[32,128]{1,0:T(8,128)} copy-done((f32[32,128]{1,0:T(8,128)}, f32[32,128]{1,0:T(8,128)S(1)}, u32[]{:S(2)}) %copy-start.1) | copy-done | bytes 16408
  17.1 0.0 copy-start.2
  17.1 0.6 %copy-done.2 = f32[32,128]{1,0:T(8,128)} copy-done((f32[32,128]{1,0:T(8,128)}, f32[32,128]{1,0:T(8,128)S(1)}, u32[]{:S(2)}) %copy-start.2) | copy-done | bytes 16408
  17.7 2.1 %shard_map.104 = bf16[16,48,128]{2,1,0:T(8,128)(2,1)} custom-call(f32[1024,128]{1,0:T(8,128)} %shard_map.103.f_ref, f32[32,128]{1,0:T(8,128)} %copy-done.1, f32[32,128]{1,0:T(8,128)} %copy-done.2, bf16[4,32,128]{2,1,0:T(8,128)(2,1)} %constant.22.clone.refs_2_, bf16[4,3,48,128]{3,2,1,0:T(8,128)(2,1)} %constant.23.clone.refs_3_), custom_call_target="tpu_custom_call" | custom-call | flops 10000000 | bytes 933888 | tf_op jit(solution)/shard_map/pallas_call | solution.py:134
Async XLA Ops:
  1.8 4.3 %collective-permute-start = (f32[80,128]{1,0:T(8,128)}, f32[80,128]{1,0:T(8,128)S(1)}, u32[]{:S(2)}, u32[]{:S(2)}) collective-permute-start(f32[80,128]{1,0:T(8,128)} %shard_map.101), channel_id=1, source_target_pairs={{0,16},{16,0},{1,17},{17,1},{2,18},{18,2},{3,19},{19,3},{4,20},{20... | collective-permute-start | bytes 122888 | tf_op jit(solution)/shard_map/ppermute | solution.py:355
  6.1 0.6 %copy-start = (f32[80,128]{1,0:T(8,128)}, f32[80,128]{1,0:T(8,128)S(1)}, u32[]{:S(2)}) copy-start(f32[80,128]{1,0:T(8,128)S(1)} %collective-permute-done.refs_0_) | copy-start | bytes 122884
  8.9 7.6 %collective-permute-start.1 = (f32[32,128]{1,0:T(8,128)}, f32[32,128]{1,0:T(8,128)S(1)}, u32[]{:S(2)}, u32[]{:S(2)}) collective-permute-start(f32[32,128]{1,0:T(8,128)} %get-tuple-element.9), channel_id=1, source_target_pairs={{0,1},{1,0},{2,3},{3,2},{4,5},{5,4},{6,7},{7,6},{8,9},{9,8},{10,11... | collective-permute-start | bytes 49160 | tf_op jit(solution)/shard_map/ppermute | solution.py:369
  9.8 6.7 %collective-permute-start.2 = (f32[32,128]{1,0:T(8,128)}, f32[32,128]{1,0:T(8,128)S(1)}, u32[]{:S(2)}, u32[]{:S(2)}) collective-permute-start(f32[32,128]{1,0:T(8,128)} %get-tuple-element.10), channel_id=1, source_target_pairs={{1,2},{2,1},{3,4},{4,3},{5,6},{6,5},{7,8},{8,7},{9,10},{10,9},{11,... | collective-permute-start | bytes 49160 | tf_op jit(solution)/shard_map/ppermute | solution.py:369
  16.5 0.6 %copy-start.1 = (f32[32,128]{1,0:T(8,128)}, f32[32,128]{1,0:T(8,128)S(1)}, u32[]{:S(2)}) copy-start(f32[32,128]{1,0:T(8,128)S(1)} %collective-permute-done.1.refs_0_) | copy-start | bytes 49156
  17.1 0.6 %copy-start.2 = (f32[32,128]{1,0:T(8,128)}, f32[32,128]{1,0:T(8,128)S(1)}, u32[]{:S(2)}) copy-start(f32[32,128]{1,0:T(8,128)S(1)} %collective-permute-done.2.refs_1_) | copy-start | bytes 49156

commit v2 on v1

--- a/solution.py
+++ b/solution.py
@@ -126,19 +126,30 @@
 
 NN, NT, TN = ((1,), (0,)), ((1,), (1,)), ((0,), (0,))
 VMEM = pl.BlockSpec(memory_space=pltpu.VMEM)
-
-
-def call(kernel, outs, args, scratch=(), flops=0, specs=None):
+HBM = pl.BlockSpec(memory_space=pltpu.HBM)
+
+
+def call(kernel, outs, args, scratch=(), flops=0, hbm=0):
     moved = sum(int(np.prod(a.shape)) * a.dtype.itemsize for a in list(args) + list(outs))
     many = len(outs) > 1
+    stay = len(args) - hbm
+    args = list(args[:stay]) + [pltpu.with_memory_space_constraint(a, pltpu.HBM) for a in args[stay:]]
     return pl.pallas_call(
         kernel,
         out_shape=tuple(outs) if many else outs[0],
-        in_specs=specs or [VMEM] * len(args),
+        in_specs=[VMEM] * stay + [HBM] * hbm,
         out_specs=(VMEM,) * len(outs) if many else VMEM,
         scratch_shapes=list(scratch),
         cost_estimate=pl.CostEstimate(flops=flops, bytes_accessed=moved, transcendentals=0),
+        compiler_params=pltpu.CompilerParams(vmem_limit_bytes=8 << 20),
     )(*args)
+
+
+def fetch(sem, *pairs):
+    copies = [pltpu.make_async_copy(a, b, sem.at[i]) for i, (a, b) in enumerate(pairs)]
+    for c in copies:
+        c.start()
+    return copies
 
 
 def body_of(ny, nx):
@@ -220,8 +231,13 @@
             out = mm(jnp.concatenate([hi, lo], 0), q, NN)
             return out[: mat.shape[0]] + out[mat.shape[0] :]
 
-        def k_send_y(q_ref, s_ref, v_ref, *outs):
-            v = v_ref[yplan.kind("grp")]
+        def k_send_y(q_hbm, s_hbm, v_hbm, y_hbm, *refs):
+            outs, (q_ref, s_ref, y_ref, v_ref, sem) = refs[: len(ey)], refs[len(ey) :]
+            p = yplan.kind("grp")
+            copies = fetch(sem, (q_hbm, q_ref), (s_hbm, s_ref), (v_hbm.at[p], v_ref), (y_hbm.at[p], y_ref))
+            for c in copies[:3]:
+                c.wait()
+            v = v_ref[...]
             part = [scaled(v, s_ref[0, z : z + 1, :], q_ref[z]) for z in range(nz)]
             for l in lv:
                 part = lift_planes(part)
@@ -234,9 +250,14 @@
             for e in ey:
                 if mrows[e] > mbase[e][-1]:
                     outs[e][mbase[e][-1] :, :] = jnp.zeros((mrows[e] - mbase[e][-1], LANES), f32)
-
-        def k_own_yz(q_ref, s_ref, y_ref, d_ref, t_ref):
-            y = y_ref[yplan.kind("grp")]
+            copies[3].wait()
+
+        def k_own_yz(q_ref, s_ref, y_ref, *refs):
+            tables, (d_ref, *kept), (t_ref, sem) = refs[:ntab], refs[ntab : 2 * ntab + 1], refs[2 * ntab + 1 :]
+            p, px = yplan.kind("grp"), xplan.kind("tile")
+            kinds = [p] + [px] * (ntab - 1)
+            copies = fetch(sem, *[(t.at[i], k) for t, i, k in zip(tables, kinds, kept)])
+            y = y_ref[...]
             for z in range(nz):
                 t_ref[z] = scaled(y, s_ref[0, z : z + 1, :], q_ref[z])
             for l in lv:
@@ -251,15 +272,16 @@
                         d_ref[o : o + n, :] = part[k][:n]
             if total > base[-1]:
                 d_ref[base[-1] :, :] = jnp.zeros((total - base[-1], LANES), f32)
+            for c in copies:
+                c.wait()
 
         def k_send_x(d_ref, *refs):
             ms, (u_ref, s0_ref, s1_ref) = refs[: len(ey)], refs[len(ey) : len(ey) + 3]
             o_ref, outs = refs[len(ey) + 3], refs[len(ey) + 4 :]
-            p = yplan.kind("grp")
             for l in lv:
                 for t in range(0, height[l], 8):
                     n = min(8, height[l] - t)
-                    u = u_ref[p, yoff[l] + t : yoff[l] + t + n, :]
+                    u = u_ref[yoff[l] + t : yoff[l] + t + n, :]
                     cs = {(e, i): u[:, 8 * e + i : 8 * e + i + 1] for e in ey for i in range(yplan.rank[e][l])}
                     cs = {key: jnp.broadcast_to(c, (n, LANES)) for key, c in cs.items()}
                     for k in range(planes[l]):
@@ -271,8 +293,7 @@
                         o_ref[o : o + n, :] = acc
             if total > base[-1]:
                 o_ref[base[-1] :, :] = jnp.zeros((total - base[-1], LANES), f32)
-            px = xplan.kind("tile")
-            a0, a1 = s0_ref[px], s1_ref[px]
+            a0, a1 = s0_ref[...], s1_ref[...]
             a0, a1 = jnp.concatenate([a0, a0], 1), jnp.concatenate([a1, a1], 1)
             lane = lax.broadcasted_iota(jnp.int32, (8, LANES), 1)
             for c in range(chunks):
@@ -296,19 +317,15 @@
                 if xrows0 > r0 * chunks0:
                     outs[e][r0 * chunks0 : xrows0, :] = jnp.zeros((xrows0 - r0 * chunks0, LANES), f32)
 
-        def k_own_x(d_ref, x_ref, o_ref, x_vmem, sem):
-            copy = pltpu.make_async_copy(x_ref.at[xplan.kind("tile")], x_vmem, sem)
-            copy.start()
-            copy.wait()
+        def k_own_x(d_ref, x_ref, o_ref):
             for l in lv:
                 end = base[l + 1] if l + 1 < LEVELS else total
                 hi, lo = split(d_ref[base[l] : end, :])
-                o_ref[base[l] : end, :] = mm(jnp.concatenate([hi, lo, hi], 1), x_vmem[l], NN)
+                o_ref[base[l] : end, :] = mm(jnp.concatenate([hi, lo, hi], 1), x_ref[l], NN)
 
         def k_join(f_ref, *refs):
             ms, (u0_ref, u1_ref, out_ref, acc, low) = refs[: len(ex)], refs[len(ex) :]
-            px = xplan.kind("tile")
-            u0 = u0_ref[px]
+            u0 = u0_ref[...]
             for c in range(chunks0):
                 rows_in = [ms[e][r0 * c : r0 * (c + 1), :] for e in ex]
                 if k0 > ne * r0:
@@ -332,7 +349,7 @@
                     end = base[l + 1] if l + 1 < LEVELS else total
                     b = min(end, (c + 1) * LANES)
                     if a < b:
-                        m = mm(lhs, u1_ref[px, l - 1], TN)
+                        m = mm(lhs, u1_ref[l - 1], TN)
                         low[a - base[1] : b - base[1], :] = f_ref[a:b, :] + m[a - c * LANES : b - c * LANES]
             for l in range(1, LEVELS):
                 step, h = 1 << l, height[l]
@@ -345,41 +362,41 @@
                 out_ref[z] = acc[z * rows : (z + 1) * rows, :].astype(bf16)
 
         shape = jax.ShapeDtypeStruct
-        sent = call(
+        like = lambda a: shape(a.shape, a.dtype)
+        one = lambda a: shape(a.shape[1:], a.dtype)
+        xtab = tab(xown.reshape(xplan.kinds, LEVELS, 3 * LANES, LANES), bf16)
+        tables = [tab(ucoef, f32), tab(s0, bf16), tab(s1, bf16), xtab, tab(ur0, bf16), tab(ur1, bf16)]
+        ntab = len(tables)
+        vtab, ytab = tab(vmat, f32), tab(yown, f32)
+        *sent, q, s, y = call(
             k_send_y,
-            [shape((mrows[e], LANES), f32) for e in ey],
-            [quantized, scales, tab(vmat, f32)],
+            [shape((mrows[e], LANES), f32) for e in ey] + [like(quantized), like(scales), one(ytab)],
+            [quantized, scales, vtab, ytab],
+            [pltpu.VMEM(vtab.shape[1:], f32), pltpu.SemaphoreType.DMA((4,))],
             flops=1000000,
+            hbm=4,
         )
-        sent = sent if isinstance(sent, (tuple, list)) else [sent]
         got = [lax.ppermute(sent[e], "grp", yplan.perms[e]) for e in ey]
-        d = call(
+        d, u, a0, a1, xt, u0, u1 = call(
             k_own_yz,
-            [shape((total, LANES), f32)],
-            [quantized, scales, tab(yown, f32)],
-            [pltpu.VMEM((nz, yoff[-1], LANES), f32)],
+            [shape((total, LANES), f32)] + [one(t) for t in tables],
+            [q, s, y, *tables],
+            [pltpu.VMEM((nz, yoff[-1], LANES), f32), pltpu.SemaphoreType.DMA((ntab,))],
             flops=100000000,
+            hbm=ntab,
         )
         d, *sent = call(
             k_send_x,
             [shape((total, LANES), f32)] + [shape((xmsg, LANES), f32) for e in ex],
-            [d, *got, tab(ucoef, f32), tab(s0, bf16), tab(s1, bf16)],
+            [d, *got, u, a0, a1],
             flops=10000000,
         )
-        got = [lax.ppermute(sent[e], "tile", xplan.perms[e]) for e in ex]
-        xtab = tab(xown.reshape(xplan.kinds, LEVELS, 3 * LANES, LANES), bf16)
-        full = call(
-            k_own_x,
-            [shape((total, LANES), f32)],
-            [d, xtab],
-            [pltpu.VMEM((LEVELS, 3 * LANES, LANES), bf16), pltpu.SemaphoreType.DMA],
-            flops=100000000,
-            specs=[VMEM, pl.BlockSpec(memory_space=pl.ANY)],
-        )
+        got = [lax.ppermute(sent[e], "tile", xplan.perms[e]) for e in reversed(ex)][::-1]
+        full = call(k_own_x, [shape((total, LANES), f32)], [d, xt], flops=100000000)
         return call(
             k_join,
             [shape(quantized.shape, bf16)],
-            [full, *got, tab(ur0, bf16), tab(ur1, bf16)],
+            [full, *got, u0, u1],
             [pltpu.VMEM((base[1], LANES), f32), pltpu.VMEM((total - base[1], LANES), f32)],
             flops=10000000,
         )

time: 20.1 us -> 13.5 us (0.67)
  the two profiles are of different devices: /device:TPU:1 before, /device:TPU:21 now
where the time goes in v2:
time: 13.5 us; the launch traced here: 13.3 us
  starting transfers between devices  6.22 us (46%)
  Pallas kernels  4.27 us (32%)
  waiting for transfers between devices  2.81 us (21%)
    ppermute x2, starting transfers between devices, body(): lax.ppermute(sent[e], 'tile', xplan.perms[e])  4.94 us
    pallas_call x5, Pallas kernels, call(): pl.pallas_call(kernel, out_shape=tuple(outs) if many else outs[0], in_spe...  4.27 us
    ppermute x2, waiting for transfers between devices, body(): lax.ppermute(sent[e], 'tile', xplan.perms[e])  2.52 us
    ppermute x1, starting transfers between devices, body(): got = [lax.ppermute(sent[e], 'grp', yplan.perms[e]) for e in ey]  1.28 us
    ppermute x1, waiting for transfers between devices, body(): got = [lax.ppermute(sent[e], 'grp', yplan.perms[e]) for e in ey]  0.3 us
  transfers between devices with their start and end apart: 3, of which 2 were waited for; matrix products, arithmetic and copies ran while one was open for 0% of the time, Pallas kernels for 13%

profile of v2, /device:TPU:21, one launch (start us, length us, event | category | flops | bytes accessed | tf_op | source)
XLA Modules:
  0.0 13.3 jit_solution(9229989988347316853)
XLA Ops:
  0.0 1.2 %shard_map.100 = (f32[80,128]{1,0:T(8,128)S(1)}, bf16[16,48,128]{2,1,0:T(8,128)(2,1)S(1)}, f32[1,16,48]{2,1,0:T(8,128)S(1)}, f32[96,48]{1,0:T(8,128)S(1)}) custom-call(bf16[16,48,128]{2,1,0:T(8,128)(2,1)} %q_hbm.1, f32[1,16,48]{2,1,0:T(8,128)} %s_hbm.1, f32[2,16,48]{2,1,0:T(8,128)} %constant.22.clone.v_hbm, f32[2,96,48]{2,1,0:T(8,128)} %constant.23.clone.y_hbm), custom_call_target="tpu_custom_call" | custom-call | flops 1000000 | bytes 501760 | tf_op jit(solution)/shard_map/pallas_call | solution.py:137
  1.2 1.3 %collective-permute-start = (f32[80,128]{1,0:T(8,128)S(1)}, f32[80,128]{1,0:T(8,128)S(1)}, u32[]{:S(2)}, u32[]{:S(2)}) collective-permute-start(f32[80,128]{1,0:T(8,128)S(1)} %get-tuple-element.23), channel_id=1, source_target_pairs={{0,16},{16,0},{1,17},{17,1},{2,18},{18,2},{3,19},{19,3},{4,20},{20... | collective-permute-start | bytes 122888 | tf_op jit(solution)/shard_map/ppermute | solution.py:379
  2.5 1.3 %shard_map.101 = (f32[1024,128]{1,0:T(8,128)S(1)}, f32[96,128]{1,0:T(8,128)S(1)}, bf16[16,128]{1,0:T(8,128)(2,1)S(1)}, bf16[96,128]{1,0:T(8,128)(2,1)S(1)}, bf16...) custom-call(bf16[16,48,128]{2,1,0:T(8,128)(2,1)S(1)} %get-tuple-element.19.q_ref, ...), custom_call_target="tpu_custom_call" | custom-call | flops 100000000 | bytes 3224576 | tf_op jit(solution)/shard_map/pallas_call | solution.py:137
  3.8 0.3 %collective-permute-done.refs_0_ = f32[80,128]{1,0:T(8,128)S(1)} collective-permute-done((f32[80,128]{1,0:T(8,128)S(1)}, f32[80,128]{1,0:T(8,128)S(1)}, u32[]{:S(2)}, u32[]{:S(2)}) %collective-permute-start) | collective-permute-done | bytes 40992 | tf_op jit(solution)/shard_map/ppermute | solution.py:379
  4.1 0.4 %shard_map.102 = (f32[1024,128]{1,0:T(8,128)S(1)}, f32[32,128]{1,0:T(8,128)S(1)}, f32[32,128]{1,0:T(8,128)S(1)}) custom-call(f32[1024,128]{1,0:T(8,128)S(1)} %get-tuple-element.22.d_ref, f32[80,128]{1,0:T(8,128)S(1)} %collective-permute-done.refs_0_, f32[96,128]{1,0:T(8,128)S(1)} %get-tuple-element.24.refs_1_, ...), custom_call_target="tpu_custom_call" | custom-call | flops 10000000 | bytes 1200128 | tf_op jit(solution)/shard_map/pallas_call | solution.py:137
  4.5 1.9 %collective-permute-start.1 = (f32[32,128]{1,0:T(8,128)S(1)}, f32[32,128]{1,0:T(8,128)S(1)}, u32[]{:S(2)}, u32[]{:S(2)}) collective-permute-start(f32[32,128]{1,0:T(8,128)S(1)} %get-tuple-element.29), channel_id=1, source_target_pairs={{0,1},{1,0},{2,3},{3,2},{4,5},{5,4},{6,7},{7,6},{8,9},{9,8},{10,11... | collective-permute-start | bytes 49160 | tf_op jit(solution)/shard_map/ppermute | solution.py:394
  6.4 3.0 %collective-permute-start.2 = (f32[32,128]{1,0:T(8,128)S(1)}, f32[32,128]{1,0:T(8,128)S(1)}, u32[]{:S(2)}, u32[]{:S(2)}) collective-permute-start(f32[32,128]{1,0:T(8,128)S(1)} %get-tuple-element.30), channel_id=1, source_target_pairs={{1,2},{2,1},{3,4},{4,3},{5,6},{6,5},{7,8},{8,7},{9,10},{10,9},{11,... | collective-permute-start | bytes 49160 | tf_op jit(solution)/shard_map/ppermute | solution.py:394
  9.5 0.4 %shard_map.103.f_ref = f32[1024,128]{1,0:T(8,128)S(1)} custom-call(f32[1024,128]{1,0:T(8,128)S(1)} %get-tuple-element.27.d_ref, bf16[4,384,128]{2,1,0:T(8,128)(2,1)S(1)} %get-tuple-element.28.x_ref), custom_call_target="tpu_custom_call" | custom-call | flops 100000000 | bytes 1441792 | tf_op jit(solution)/shard_map/pallas_call | solution.py:137
  9.8 0.0 collective-permute-done.1.refs_0_
  9.8 2.5 %collective-permute-done.2.refs_1_ = f32[32,128]{1,0:T(8,128)S(1)} collective-permute-done((f32[32,128]{1,0:T(8,128)S(1)}, f32[32,128]{1,0:T(8,128)S(1)}, u32[]{:S(2)}, u32[]{:S(2)}) %collective-permute-start.2) | collective-permute-done | bytes 16416 | tf_op jit(solution)/shard_map/ppermute | solution.py:394
  12.4 1.0 %shard_map.104 = bf16[16,48,128]{2,1,0:T(8,128)(2,1)} custom-call(f32[1024,128]{1,0:T(8,128)S(1)} %shard_map.103.f_ref, f32[32,128]{1,0:T(8,128)S(1)} %collective-permute-done.1.refs_0_, f32[32,128]{1,0:T(8,128)S(1)} %collective-permute-done.2.refs_1_, bf16[32,128]{1,0:T(8,128)(2,1)S(1)} %get-tuple-element.31.refs_2_, ...), custom_call_target="tpu_custom_call" | custom-call | flops 10000000 | bytes 798720 | tf_op jit(solution)/shard_map/pallas_call | solution.py:137
Async XLA Ops:
  1.2 2.9 %collective-permute-start = (f32[80,128]{1,0:T(8,128)S(1)}, f32[80,128]{1,0:T(8,128)S(1)}, u32[]{:S(2)}, u32[]{:S(2)}) collective-permute-start(f32[80,128]{1,0:T(8,128)S(1)} %get-tuple-element.23), channel_id=1, source_target_pairs={{0,16},{16,0},{1,17},{17,1},{2,18},{18,2},{3,19},{19,3},{4,20},{20... | collective-permute-start | bytes 122888 | tf_op jit(solution)/shard_map/ppermute | solution.py:379
  4.5 5.3 %collective-permute-start.1 = (f32[32,128]{1,0:T(8,128)S(1)}, f32[32,128]{1,0:T(8,128)S(1)}, u32[]{:S(2)}, u32[]{:S(2)}) collective-permute-start(f32[32,128]{1,0:T(8,128)S(1)} %get-tuple-element.29), channel_id=1, source_target_pairs={{0,1},{1,0},{2,3},{3,2},{4,5},{5,4},{6,7},{7,6},{8,9},{9,8},{10,11... | collective-permute-start | bytes 49160 | tf_op jit(solution)/shard_map/ppermute | solution.py:394
  6.4 5.9 %collective-permute-start.2 = (f32[32,128]{1,0:T(8,128)S(1)}, f32[32,128]{1,0:T(8,128)S(1)}, u32[]{:S(2)}, u32[]{:S(2)}) collective-permute-start(f32[32,128]{1,0:T(8,128)S(1)} %get-tuple-element.30), channel_id=1, source_target_pairs={{1,2},{2,1},{3,4},{4,3},{5,6},{6,5},{7,8},{8,7},{9,10},{10,9},{11,... | collective-permute-start | bytes 49160 | tf_op jit(solution)/shard_map/ppermute | solution.py:394
